TPU v7x, 32 devices: a whole 2x2x4 slice. The times are simulated.
32 devices in a mesh: dp: 16 (over z, y, x), feat: 2 (over core).
Axes of the slice: x: 2, y: 2, z: 4, core: 2. Of those that a mesh axis runs over, the one named last changes fastest.
Arguments:
- samples: bfloat16 [4096, 16384], P('dp', 'feat'), may hold values from -1 to 1
- labels: int32 [4096], P('dp'), may hold values from -1 to 1, as said below
- dual: float32 [4096], P('dp'), may hold values from 0 to 1
- counts: int32 [16], P('dp'), may hold values from 1 to 2, as said below
- order: int32 [16, 2], P('dp'), may hold values from 0 to 1, each once within a row
- weights: float32 [16384], P('feat'), may hold values from -0.046875 to 0.046875
Outputs:
- weights_new: float32 [16384], P('feat')
- dual_new: float32 [4096], P('dp')
- margins: float32 [4096], P('dp')
- gap: float32 [], replicated
Inputs may be any that keep to these rules, and one draw needn't show every extreme that they name: `labels`: each entry is -1 or 1. `counts`: some index of dp has exactly 2 live blocks.
All inputs are finite; a program needn't handle non-finite values.
Results may differ from a plain program's by a relative error of at most 0.003.
Values sent between devices are 32-bit elements; how exact they have to be, the bound alone decides.
A program may use at most 64 MiB of HBM per device.

v0:
```python
import jax
import jax.numpy as jnp
from jax import lax
from jax.sharding import PartitionSpec as P

BLOCK = 128
CAP = 2
PASSES = 2


def block_solve(system, right):
    factor = jnp.linalg.cholesky(system)
    lower_part = lax.linalg.triangular_solve(factor, right[:, None], left_side=True, lower=True)
    result = lax.linalg.triangular_solve(
        factor, lower_part, left_side=True, lower=True, transpose_a=True
    )
    return result[:, 0]


def body(samples, labels, dual, counts, order, weights):
    reg = 1.0 / 384.0
    groups = lax.axis_size("dp")
    half = samples.shape[1]
    blocks_x = samples.reshape(CAP, BLOCK, half)
    total = lax.psum(counts[0].astype(jnp.float32), "dp") * BLOCK
    scale = groups / (reg * total)
    count = counts[0]
    partial_grams = jnp.einsum(
        "brd,bsd->brs", blocks_x, blocks_x, preferred_element_type=jnp.float32
    )
    grams = lax.psum(partial_grams, "feat")

    def advance(step, carry):
        beta, change = carry
        slot = order[0, step % CAP]
        rows = lax.dynamic_index_in_dim(blocks_x, slot, 0, keepdims=False)
        vector = (weights + change).astype(jnp.bfloat16)
        partial_margin = jnp.dot(rows, vector, preferred_element_type=jnp.float32)
        margin = lax.psum(partial_margin, "feat")
        gram = lax.dynamic_index_in_dim(grams, slot, 0, keepdims=False)
        start = slot * BLOCK
        signs = lax.dynamic_slice_in_dim(labels, start, BLOCK).astype(jnp.float32)
        before = lax.dynamic_slice_in_dim(beta, start, BLOCK)
        system = (
            jnp.eye(BLOCK, dtype=jnp.float32) + scale * (signs[:, None] * signs[None, :]) * gram
        )
        delta = block_solve(system, 1.0 - before - signs * margin)
        after = jnp.where(slot < count, jnp.maximum(before + delta, 0.0), before)
        scaled = (signs * (after - before)).astype(jnp.bfloat16)
        change = change + scale * jnp.dot(scaled, rows, preferred_element_type=jnp.float32)
        beta = lax.dynamic_update_slice_in_dim(beta, after, start, 0)
        return (beta, change)

    beta, change = lax.fori_loop(0, PASSES * CAP, advance, (dual, jnp.zeros((half,), jnp.float32)))
    summed = lax.psum(change, "dp")
    weights_new = weights + summed / groups
    first_group = (lax.axis_index("dp") == 0).astype(jnp.float32)
    norm_part = jnp.sum(weights_new * weights_new) * first_group
    partial_scores = jnp.dot(
        samples, weights_new.astype(jnp.bfloat16), preferred_element_type=jnp.float32
    )
    margins = lax.psum(partial_scores, "feat")
    slots = jnp.arange(CAP * BLOCK, dtype=jnp.int32)
    live = slots // BLOCK < count
    signs = labels.astype(jnp.float32)
    hinge = jnp.maximum(1.0 - signs * margins, 0.0)
    first_half = (lax.axis_index("feat") == 0).astype(jnp.float32)
    loss_part = jnp.sum(jnp.where(live, 0.5 * hinge * hinge, 0.0)) * first_half
    dual_part = jnp.sum(jnp.where(live, beta - 0.5 * beta * beta, 0.0)) * first_half
    loss, dualsum, norm = lax.psum((loss_part, dual_part, norm_part), ("dp", "feat"))
    gap = reg * norm + (loss - dualsum) / total
    return (weights_new, beta, margins, gap)


def solution(mesh):
    return jax.shard_map(
        body,
        mesh=mesh,
        in_specs=(P("dp", "feat"), P("dp"), P("dp"), P("dp"), P("dp", None), P("feat")),
        out_specs=(P("feat"), P("dp"), P("dp"), P()),
        check_vma=False,
    )
```

profile of v0, /device:TPU:0, one launch (start us, length us, event | category | flops | bytes accessed | tf_op | source)
XLA Modules:
  0.0 334.6 jit_solution(18046364474905601856)
XLA Ops:
  7.3 5.4 %fusion.36 = f32[2,128,128]{2,1,0:T(8,128)} fusion(bf16[2,128,8192]{2,1,0:T(8,128)(2,1)} %bitcast.91), kind=kOutput, calls=%fused_computation.55 | convolution fusion | flops 536870912 | bytes 4325376 | tf_op jit(solution)/shard_map/brd,bsd->brs/dot_general | solution.py:28
  13.3 44.1 %psum.63 = f32[]{:T(128)} all-reduce(f32[]{:T(128)S(6)} %convert_element_type.51), channel_id=1, replica_groups=mesh['dp'=16,'feat'=2] {'dp'}, use_global_device_ids=true, to_apply=%region_1.0 | all-reduce | flops 1 | bytes 8 | tf_op jit(solution)/shard_map/psum | solution.py:25
  58.1 147.6 %while.18 = (s32[]{:T(128)}, f32[256]{0:T(256)S(1)}, f32[8192]{0:T(1024)S(1)}, s32[1,2]{1,0:T(1,128)S(1)}, s32[]{:T(128)}, /*index=5*/f32[]{:T(128)}, s32[256]{0...) while((s32[]{:T(128)}, f32[256]{0:T(256)S(1)}, ...), condition=%wide.region_6.7_spmd.clone, body=%wide.region_2.6_spmd.clone.sunk | while | flops 4982547 | bytes 5255052 | solution.py:54
  63.4 11.7 %cholesky.78 = f32[128,128]{1,0:T(8,128)S(1)} custom-call(f32[128,128]{1,0:T(8,128)S(1)} %fusion.67), custom_call_target="Cholesky" | custom-call | tf_op jit(solution)/shard_map/while/body/eval_jaxpr/jit(cholesky)/cholesky | solution.py:12
  76.4 9.8 %custom-call.25 = f32[1,128,128]{1,2,0:T(8,128)S(1)} custom-call(f32[1,128,128]{2,1,0:T(8,128)S(1)} %fusion.68), custom_call_target="InvertDiagBlocksLowerTriangular" | custom-call | tf_op jit(solution)/shard_map/while/body/eval_jaxpr/triangular_solve | solution.py:14
  86.3 2.2 fusion.69
  88.5 2.5 psum.72
  100.3 11.7 %cholesky.78 = f32[128,128]{1,0:T(8,128)S(1)} custom-call(f32[128,128]{1,0:T(8,128)S(1)} %fusion.67), custom_call_target="Cholesky" | custom-call | tf_op jit(solution)/shard_map/while/body/eval_jaxpr/jit(cholesky)/cholesky | solution.py:12
  113.3 9.8 %custom-call.25 = f32[1,128,128]{1,2,0:T(8,128)S(1)} custom-call(f32[1,128,128]{2,1,0:T(8,128)S(1)} %fusion.68), custom_call_target="InvertDiagBlocksLowerTriangular" | custom-call | tf_op jit(solution)/shard_map/while/body/eval_jaxpr/triangular_solve | solution.py:14
  123.2 2.2 fusion.69
  125.4 2.5 psum.72
  129.6 2.1 fusion.71
  137.2 11.7 %cholesky.78 = f32[128,128]{1,0:T(8,128)S(1)} custom-call(f32[128,128]{1,0:T(8,128)S(1)} %fusion.67), custom_call_target="Cholesky" | custom-call | tf_op jit(solution)/shard_map/while/body/eval_jaxpr/jit(cholesky)/cholesky | solution.py:12
  150.2 9.8 %custom-call.25 = f32[1,128,128]{1,2,0:T(8,128)S(1)} custom-call(f32[1,128,128]{2,1,0:T(8,128)S(1)} %fusion.68), custom_call_target="InvertDiagBlocksLowerTriangular" | custom-call | tf_op jit(solution)/shard_map/while/body/eval_jaxpr/triangular_solve | solution.py:14
  160.1 2.2 fusion.69
  162.3 2.5 psum.72
  174.1 11.7 %cholesky.78 = f32[128,128]{1,0:T(8,128)S(1)} custom-call(f32[128,128]{1,0:T(8,128)S(1)} %fusion.67), custom_call_target="Cholesky" | custom-call | tf_op jit(solution)/shard_map/while/body/eval_jaxpr/jit(cholesky)/cholesky | solution.py:12
  187.1 9.8 %custom-call.25 = f32[1,128,128]{1,2,0:T(8,128)S(1)} custom-call(f32[1,128,128]{2,1,0:T(8,128)S(1)} %fusion.68), custom_call_target="InvertDiagBlocksLowerTriangular" | custom-call | tf_op jit(solution)/shard_map/while/body/eval_jaxpr/triangular_solve | solution.py:14
  197.0 2.2 fusion.69
  199.2 2.5 psum.72
  205.7 71.7 %psum.65 = f32[8192]{0:T(1024)S(1)} all-reduce(f32[8192]{0:T(1024)S(1)} %get-tuple-element.248), channel_id=1, replica_groups=mesh['dp'=16,'feat'=2] {'dp'}, use_global_device_ids=true, to_apply=%region_7.8 | all-reduce | flops 8192 | bytes 65536 | tf_op jit(solution)/shard_map/psum | solution.py:55
  278.1 3.4 %fusion.37 = f32[1,256]{1,0:T(1,128)S(1)} fusion(bf16[8192,1]{0,1:T(2,128)(2,1)S(1)} %reshape.63, bf16[256,8192]{1,0:T(8,128)(2,1)} %bitcast.93), kind=kOutput, calls=%fused_computation.56 | convolution fusion | flops 4194304 | bytes 4211712 | tf_op jit(solution)/shard_map/dot_general | solution.py:59
  281.5 2.5 psum.66
  287.7 36.9 %all-reduce = (f32[]{:T(128)}, f32[]{:T(128)}, f32[]{:T(128)}) all-reduce(f32[]{:T(128)S(6)} %mul.160, f32[]{:T(128)S(6)} %mul.165, f32[]{:T(128)S(6)} %mul.168), channel_id=1, replica_groups=mesh['dp'=16,'feat'=2] {'dp','feat'}, use_global_device_ids=true, to_apply=%region_10.11 | all-reduce | flops 3 | bytes 24 | tf_op jit(solution)/shard_map/psum | solution.py:70
  (82 shorter events, 26.7 us)
Async XLA Ops:
  7.2 50.9 %all-reduce.3.cloned.1.call-start = ((), (), s32[]{:S(2)}) async-start(), calls=%async_computation | async-start | bytes 262144 | tf_op jit(solution)/shard_map/psum | solution.py:31
  7.2 50.9 %copy-start = (f32[8192]{0:T(1024)S(1)}, f32[8192]{0:T(1024)}, u32[]{:S(2)}) copy-start(f32[8192]{0:T(1024)} %param.13) | copy-start | bytes 98308
  7.2 50.9 %copy-start.3 = (f32[256]{0:T(256)S(1)}, f32[256]{0:T(256)}, u32[]{:S(2)}) copy-start(f32[256]{0:T(256)} %param.10) | copy-start | bytes 3076
  7.2 50.9 %copy-start.4 = (s32[256]{0:T(256)S(1)}, s32[256]{0:T(256)}, u32[]{:S(2)}) copy-start(s32[256]{0:T(256)} %param.9) | copy-start | bytes 3076
  7.2 50.9 %copy-start.6 = (s32[1,2]{1,0:T(1,128)S(1)}, s32[1,2]{1,0:T(1,128)}, u32[]{:S(2)}) copy-start(s32[1,2]{1,0:T(1,128)} %param.12) | copy-start | bytes 28
  205.7 120.8 %copy-start.2 = (f32[256]{0:T(256)}, f32[256]{0:T(256)S(1)}, u32[]{:S(2)}) copy-start(f32[256]{0:T(256)S(1)} %get-tuple-element.245) | copy-start | bytes 3076
  278.1 48.5 %copy-start.1 = (f32[8192]{0:T(1024)}, f32[8192]{0:T(1024)S(1)}, u32[]{:S(2)}) copy-start(f32[8192]{0:T(1024)S(1)} %get-tuple-element.307) | copy-start | bytes 98308
  283.9 42.6 %copy-start.5 = (f32[256]{0:T(256)}, f32[256]{0:T(256)S(1)}, u32[]{:S(2)}) copy-start(f32[256]{0:T(256)S(1)} %psum.66) | copy-start | bytes 3076
Sparse Core Ops, SparseCore 0:
  12.8 20.6 all-reduce.2
where the time goes:
time: 337 us; the launch traced here: 335 us
  blocking collectives  165 us (49%)
  other arithmetic  101 us (30%)
  matrix products  27.6 us (8%)
  between operations  21 us (6%)
  loops' own time  16 us (5%)
  local copies, waits for them, and re-layouts  3.78 us (1%)
    psum x1, blocking collectives, body(): summed = lax.psum(change, 'dp')  71.7 us
    another operation x12, other arithmetic, block_solve(): factor = jnp.linalg.cholesky(system)  49.6 us
    psum x1, blocking collectives, body(): total = lax.psum(counts[0].astype(jnp.float32), 'dp') * BLOCK  44.1 us
    another operation x8, other arithmetic, block_solve(): lax.linalg.triangular_solve(factor, lower_part, left_side=True, lower=Tru...  41.9 us
    psum x1, blocking collectives, body(): lax.psum((loss_part, dual_part, norm_part), ('dp', 'feat'))  36.9 us
    another operation x1, loops' own time, body(): lax.fori_loop(0, PASSES * CAP, advance, (dual, jnp.zeros((half,), jnp.flo...  16 us
    psum x4, blocking collectives, advance(): margin = lax.psum(partial_margin, 'feat')  9.85 us
    dot_general x4, matrix products, advance(): partial_margin = jnp.dot(rows, vector, preferred_element_type=jnp.float32)  8.94 us
  transfers between devices with their start and end apart: 1, of which 0 were waited for; matrix products, arithmetic and copies ran while one was open for 0% of the time, Pallas kernels for 0%

commit v1 on v0

v1 whole, which is shorter than its diff:
```python
import functools

import jax
import jax.numpy as jnp
from jax import lax
from jax.experimental import pallas as pl
from jax.experimental.pallas import tpu as pltpu
from jax.sharding import PartitionSpec as P

BLOCK = 128
CAP = 2
PASSES = 2
LANES = 128
LOAD = 1024
REG = 1.0 / 384.0
MESH = pl.DeviceIdType.MESH
F32 = jnp.float32
BF16 = jnp.bfloat16


def dot_t(a, b):
    return lax.dot_general(a, b, (((1,), (1,)), ((), ())), preferred_element_type=F32)


def dot_full(a, b):
    return lax.dot_general(
        a,
        b,
        (((1,), (0,)), ((), ())),
        preferred_element_type=F32,
        precision=lax.Precision.HIGHEST,
    )


def iterations(features):
    low = 1.0 / (1.0 + features / REG)
    count = 0
    while low < 1.0 - 1e-6:
        low = 4.0 * low / (1.0 + low) ** 2
        count += 1
    return count


def to_row(col, eye):
    return jnp.sum(jnp.where(eye, col, 0.0), axis=0, keepdims=True)


def to_col(row, eye):
    return jnp.sum(jnp.where(eye, row, 0.0), axis=1, keepdims=True)


def two_rows(first, second):
    width = first.shape[1]
    index = lax.broadcasted_iota(jnp.int32, (16, width), 0)
    wide = jnp.where(index == 0, first, jnp.where(index == 1, second, 0.0))
    return wide.astype(BF16)


def split(row):
    high = row.astype(BF16).astype(F32)
    return two_rows(high, row - high)


def kernel(
    groups,
    owners,
    rounds,
    counts_ref,
    order_ref,
    x_hbm,
    w_ref,
    y_ref,
    dual_ref,
    wn_ref,
    dn_ref,
    mg_ref,
    gap_ref,
    xs,
    gram_mine,
    gram_other,
    cnt_mine,
    cnt_all,
    u_mine,
    u_all,
    wn_mine,
    wn_all,
    f_mine,
    f_other,
    t_mine,
    t_all,
    load_sem,
    send_sem,
    recv_sem,
    fsend_sem,
    frecv_sem,
):
    me = lax.axis_index("dp")
    half_id = lax.axis_index("feat")
    partner = 1 - half_id
    rows, half = xs.shape
    chunk = half // owners
    loads = half // LOAD

    def load(i):
        cols = pl.ds(i * LOAD, LOAD)
        return pltpu.make_async_copy(x_hbm.at[:, cols], xs.at[:, cols], load_sem.at[i])

    for i in range(loads):
        load(i).start()

    barrier = pltpu.get_barrier_semaphore()

    def greet(k, _):
        pl.semaphore_signal(
            barrier, inc=1, device_id={"dp": lax.rem(me + k, groups)}, device_id_type=MESH
        )
        return 0

    lax.fori_loop(1, groups, greet, 0)
    pl.semaphore_signal(barrier, inc=1, device_id={"feat": partner}, device_id_type=MESH)

    def send_to(phase, peer, src, dst):
        return pltpu.make_async_remote_copy(
            src_ref=src,
            dst_ref=dst,
            send_sem=send_sem.at[phase, peer],
            recv_sem=recv_sem.at[phase, me],
            device_id={"dp": peer},
            device_id_type=MESH,
        )

    def recv_from(phase, peer, dst):
        return pltpu.make_async_remote_copy(
            src_ref=dst,
            dst_ref=dst,
            send_sem=send_sem.at[phase, peer],
            recv_sem=recv_sem.at[phase, peer],
            device_id={"dp": peer},
            device_id_type=MESH,
        )

    def others(fn):
        def one(k, _):
            fn(lax.rem(me + k, groups))
            return 0

        lax.fori_loop(1, groups, one, 0)

    def if_owner(index, fn):
        if owners == groups:
            fn()
        else:
            pl.when(index < owners)(fn)

    count = counts_ref[0]
    cnt_mine[...] = jnp.full((1, LANES), count.astype(F32), F32)
    eye = lax.broadcasted_iota(jnp.int32, (BLOCK, BLOCK), 0) == lax.broadcasted_iota(
        jnp.int32, (BLOCK, BLOCK), 1
    )

    total = None
    for i in range(loads):
        cols = pl.ds(i * LOAD, LOAD)
        load(i).wait()
        part = xs[:, cols]
        left = jnp.concatenate([part, split(w_ref[:, cols])], axis=0)
        product = dot_t(left, part)
        total = product if total is None else total + product
    gram_mine[...] = total

    pl.semaphore_wait(barrier, groups)

    feat_copy = pltpu.make_async_remote_copy(
        src_ref=gram_mine,
        dst_ref=gram_other,
        send_sem=fsend_sem.at[0],
        recv_sem=frecv_sem.at[0],
        device_id={"feat": partner},
        device_id_type=MESH,
    )
    others(lambda p: send_to(0, p, cnt_mine, cnt_all.at[me]).start())
    feat_copy.start()

    slots = [order_ref[0, v] for v in range(CAP)]

    def pick(items, slot):
        value = items[0]
        for s in range(1, CAP):
            value = jnp.where(slot == s, items[s], value)
        return value

    y_rows = [y_ref[s : s + 1, :].astype(F32) for s in range(CAP)]
    b_rows = [dual_ref[s : s + 1, :] for s in range(CAP)]
    y_row = [pick(y_rows, slot) for slot in slots]
    b_row = [pick(b_rows, slot) for slot in slots]
    y_col = [to_col(r, eye) for r in y_row]
    b_col = [to_col(r, eye) for r in b_row]

    others(lambda p: recv_from(0, p, cnt_all.at[p]).wait_recv())
    cnt_all[me] = cnt_mine[...]
    live_blocks = lax.fori_loop(
        0, groups, lambda i, acc: acc + cnt_all[i], jnp.zeros((1, LANES), F32)
    )
    samples_total = live_blocks * BLOCK
    scale = groups / (REG * samples_total)

    feat_copy.wait()
    full = gram_mine[...] + gram_other[...]
    first = full[rows : rows + 1, :] + full[rows + 1 : rows + 2, :]
    m_rows = [first[:, s * BLOCK : (s + 1) * BLOCK] for s in range(CAP)]
    m_row = [pick(m_rows, slot) for slot in slots]

    def block(r, s):
        return full[r * BLOCK : (r + 1) * BLOCK, s * BLOCK : (s + 1) * BLOCK]

    grams = [
        [
            pick([pick([block(r, s) for s in range(CAP)], slots[b]) for r in range(CAP)], slots[a])
            for b in range(CAP)
        ]
        for a in range(CAP)
    ]

    systems, carry = [], []
    for v in range(CAP):
        system = jnp.where(eye, 1.0, 0.0) + scale * grams[v][v]
        top = jnp.max(jnp.sum(jnp.abs(system), axis=0, keepdims=True), axis=1, keepdims=True)
        low = 1.0 / top
        step = 2.0 / (1.0 + low) * low
        carry.append(step * (jnp.where(eye, 2.0, 0.0) - step * system))
        carry.append(4.0 * low / ((1.0 + low) * (1.0 + low)))
        systems.append(system)

    def improve(_, state):
        new = []
        for v in range(CAP):
            inverse, low = state[2 * v], state[2 * v + 1]
            mu = 2.0 / (1.0 + low)
            near = dot_full(systems[v], inverse)
            new.append(mu * (2.0 * inverse - mu * dot_full(inverse, near)))
            new.append(low * mu * mu)
        return tuple(new)

    carry = lax.fori_loop(1, rounds, improve, tuple(carry))
    inverses = [carry[2 * v] for v in range(CAP)]

    moved = [None] * CAP
    for j in range(PASSES * CAP):
        a = j % CAP
        margin = m_row[a]
        for b in range(CAP):
            if moved[b] is not None:
                margin = margin + scale * jnp.sum(grams[b][a] * moved[b], axis=0, keepdims=True)
        right = y_row[a] * (1.0 - b_row[a] - y_row[a] * margin)
        delta = y_col[a] * jnp.sum(inverses[a] * right, axis=1, keepdims=True)
        after = jnp.where(slots[a] < count, jnp.maximum(b_col[a] + delta, 0.0), b_col[a])
        scaled = (y_col[a] * (after - b_col[a])).astype(BF16).astype(F32)
        moved[a] = scaled if moved[a] is None else moved[a] + scaled
        b_col[a] = after
        b_row[a] = to_row(after, eye)

    def by_slot(items, s):
        value = items[0]
        for v in range(1, CAP):
            value = jnp.where(slots[v] == s, items[v], value)
        return value

    moved_row = [to_row(m, eye) for m in moved]
    beta_rows = [by_slot(b_row, s) for s in range(CAP)]
    for s in range(CAP):
        dn_ref[s : s + 1, :] = beta_rows[s]
    steps = split(jnp.concatenate([by_slot(moved_row, s) for s in range(CAP)], axis=1))

    scale_one = scale[:, 0:1]
    for i in range(owners):
        out = lax.dot_general(
            steps,
            xs[:, i * chunk : (i + 1) * chunk],
            (((1,), (0,)), ((), ())),
            preferred_element_type=F32,
        )
        u_mine[i] = scale_one * (out[0:1, :] + out[1:2, :])

        @pl.when(me != i)
        def _(i=i):
            send_to(1, i, u_mine.at[i], u_all.at[me]).start()

    def reduce_own():
        others(lambda p: recv_from(1, p, u_all.at[p]).wait_recv())
        u_all[me] = u_mine[me]
        summed = lax.fori_loop(
            0, groups, lambda i, acc: acc + u_all[i], jnp.zeros((1, chunk), F32)
        )
        mine = w_ref[:, pl.ds(pl.multiple_of(me * chunk, LANES), chunk)] + summed / groups
        wn_mine[...] = mine
        others(lambda p: send_to(2, p, wn_mine, wn_all.at[me]).start())
        wn_all[me] = mine
        norm = jnp.sum(mine * mine, axis=1, keepdims=True)
        f_mine[:, rows:] = jnp.broadcast_to(norm, (1, LANES))

    if owners != groups:
        f_mine[:, rows:] = jnp.zeros((1, LANES), F32)
    if_owner(me, reduce_own)

    scores = jnp.zeros((16, rows), F32)
    for i in range(owners):

        @pl.when(me != i)
        def _(i=i):
            recv_from(2, i, wn_all.at[i]).wait_recv()

        value = wn_all[i]
        wn_ref[i] = value
        index = lax.broadcasted_iota(jnp.int32, (16, chunk), 0)
        left = jnp.where(index == 0, value, 0.0).astype(BF16)
        scores = scores + dot_t(left, xs[:, i * chunk : (i + 1) * chunk])
    f_mine[:, :rows] = scores[0:1, :]

    margin_copy = pltpu.make_async_remote_copy(
        src_ref=f_mine,
        dst_ref=f_other,
        send_sem=fsend_sem.at[1],
        recv_sem=frecv_sem.at[1],
        device_id={"feat": partner},
        device_id_type=MESH,
    )
    margin_copy.start()
    dual_part = jnp.zeros((1, BLOCK), F32)
    for s in range(CAP):
        beta = beta_rows[s]
        dual_part = dual_part + jnp.where(s < count, beta - 0.5 * beta * beta, 0.0)
    margin_copy.wait()
    both = f_mine[...] + f_other[...]
    loss_part = jnp.zeros((1, BLOCK), F32)
    for s in range(CAP):
        margins = both[:, s * BLOCK : (s + 1) * BLOCK]
        mg_ref[s : s + 1, :] = margins
        hinge = jnp.maximum(1.0 - y_rows[s] * margins, 0.0)
        loss_part = loss_part + jnp.where(s < count, 0.5 * hinge * hinge, 0.0)
    spread = jnp.sum(loss_part - dual_part, axis=1, keepdims=True)
    t_mine[...] = REG * both[:, rows:] + spread / samples_total
    others(lambda p: send_to(3, p, t_mine, t_all.at[me]).start())
    t_all[me] = t_mine[...]
    others(lambda p: recv_from(3, p, t_all.at[p]).wait_recv())
    gap = lax.fori_loop(0, groups, lambda i, acc: acc + t_all[i], jnp.zeros((1, LANES), F32))
    gap_ref[...] = gap

    def drain(p):
        send_to(0, p, cnt_mine, cnt_all.at[me]).wait_send()
        if_owner(p, lambda: send_to(1, p, u_mine.at[p], u_all.at[me]).wait_send())
        if_owner(me, lambda: send_to(2, p, wn_mine, wn_all.at[me]).wait_send())
        send_to(3, p, t_mine, t_all.at[me]).wait_send()

    others(drain)


def body(groups, features, samples, labels, dual, counts, order, weights):
    rows, half = samples.shape
    owners = min(groups, half // LANES)
    chunk = half // owners
    vmem = pl.BlockSpec(memory_space=pltpu.VMEM)
    smem = pl.BlockSpec(memory_space=pltpu.SMEM)
    tall = rows + 16
    wn, dn, mg, gap = pl.pallas_call(
        functools.partial(kernel, groups, owners, iterations(features)),
        out_shape=(
            jax.ShapeDtypeStruct((owners, 1, chunk), F32),
            jax.ShapeDtypeStruct((CAP, BLOCK), F32),
            jax.ShapeDtypeStruct((CAP, BLOCK), F32),
            jax.ShapeDtypeStruct((1, LANES), F32),
        ),
        in_specs=[smem, smem, pl.BlockSpec(memory_space=pl.ANY), vmem, vmem, vmem],
        out_specs=(vmem, vmem, vmem, vmem),
        scratch_shapes=[
            pltpu.VMEM((rows, half), BF16),
            pltpu.VMEM((tall, rows), F32),
            pltpu.VMEM((tall, rows), F32),
            pltpu.VMEM((1, LANES), F32),
            pltpu.VMEM((groups, 1, LANES), F32),
            pltpu.VMEM((owners, 1, chunk), F32),
            pltpu.VMEM((groups, 1, chunk), F32),
            pltpu.VMEM((1, chunk), F32),
            pltpu.VMEM((owners, 1, chunk), F32),
            pltpu.VMEM((1, rows + LANES), F32),
            pltpu.VMEM((1, rows + LANES), F32),
            pltpu.VMEM((1, LANES), F32),
            pltpu.VMEM((groups, 1, LANES), F32),
            pltpu.SemaphoreType.DMA((half // LOAD,)),
            pltpu.SemaphoreType.DMA((4, groups)),
            pltpu.SemaphoreType.DMA((4, groups)),
            pltpu.SemaphoreType.DMA((2,)),
            pltpu.SemaphoreType.DMA((2,)),
        ],
        compiler_params=pltpu.CompilerParams(collective_id=0, has_side_effects=True),
    )(
        counts,
        order,
        samples,
        weights.reshape(1, half),
        labels.reshape(CAP, BLOCK),
        dual.reshape(CAP, BLOCK),
    )
    return (wn.reshape(half), dn.reshape(rows), mg.reshape(rows), gap[0, 0])


def solution(mesh):
    groups = mesh.shape["dp"]
    halves = mesh.shape["feat"]

    def run(samples, *rest):
        return body(groups, samples.shape[1] * halves, samples, *rest)

    return jax.shard_map(
        run,
        mesh=mesh,
        in_specs=(P("dp", "feat"), P("dp"), P("dp"), P("dp"), P("dp", None), P("feat")),
        out_specs=(P("feat"), P("dp"), P("dp"), P()),
        check_vma=False,
    )
```

time: 337 us -> 47 us (0.14)
  blocking collectives: 165 us -> 0 us
  other arithmetic: 101 us -> 0 us
  Pallas kernels: 0 us -> 39.9 us
  matrix products: 27.6 us -> 0 us
  between operations: 21 us -> 3.03 us
  loops' own time: 16 us -> 0 us
    psum x8 -> x0, blocking collectives: 165 us -> none  [the longest x1 71.7 us: body(): summed = lax.psum(change, 'dp')]
    another operation x20 -> x0, other arithmetic: 91.4 us -> none  [the longest x12 49.6 us: block_solve(): factor = jnp.linalg.cholesky(system)]
    pallas_call x0 -> x1, Pallas kernels: none -> 39.9 us  [body(): pl.pallas_call(functools.partial(kernel, groups, owners, iterations(featu...]
    dot_general x10 -> x0, matrix products: 26 us -> none  [the longest x4 8.94 us: advance(): partial_margin = jnp.dot(rows, vector, preferred_element_type=jnp.float32)]
    another operation x1 -> x0, loops' own time: 16 us -> none  [body(): lax.fori_loop(0, PASSES * CAP, advance, (dual, jnp.zeros((half,), jnp.flo...]
    unnamed x14 -> x3, local copies, waits for them, and re-layouts: 0.03 us -> 3.8 us
    add x8 -> x0, other arithmetic: 3.75 us -> none  [the longest x4 3.71 us: advance(): jnp.eye(BLOCK, dtype=jnp.float32)]
    div x4 -> x0, other arithmetic: 3.73 us -> none  [block_solve(): factor = jnp.linalg.cholesky(system)]
  transfers between devices with their start and end apart: 1 -> 0, of which waited for: 0 -> 0; matrix products, arithmetic and copies ran while one was open for 0% -> 0% of each run, Pallas kernels for 0% -> 0%
where the time goes in v1:
time: 47 us; the launch traced here: 46.7 us
  Pallas kernels  39.9 us (85%)
  local copies, waits for them, and re-layouts  3.8 us (8%)
  between operations  3.03 us (6%)
    pallas_call x1, Pallas kernels, body(): pl.pallas_call(functools.partial(kernel, groups, owners, iterations(featu...  39.9 us
    unnamed x3, local copies, waits for them, and re-layouts  3.8 us

profile of v1, /device:TPU:0, one launch (start us, length us, event | category | flops | bytes accessed | tf_op | source)
XLA Modules:
  0.0 46.7 jit_solution(11590795411095757207)
XLA Ops:
  1.3 39.9 %shard_map.93 = (f32[16,1,512]{2,1,0:T(1,128)}, f32[2,128]{1,0:T(2,128)}, f32[2,128]{1,0:T(2,128)}, f32[1,128]{1,0:T(1,128)}) custom-call(s32[1]{0:T(128)S(6)} %copy.14.counts_ref, s32[1,2]{1,0:T(1,128)} %order_ref.1, bf16[256,8192]{1,0:T(8,128)(2,1)} %x_hbm.1, f32[1,8192]{1,0:T(1,128)} %bitcast.8, s32[2,128]{1,0:T(2,128)} %bitcast.10, f32[2,128]{1,0:T(2,128)} %bitcast.11), custom_call_target="tpu_custom_call" | custom-call | tf_op jit(solution)/shard_map/pallas_call | solution.py:364
  41.1 1.4 %copy.15 = f32[8192]{0:T(1024)} copy(f32[8192]{0:T(1024)} %bitcast.9) | data formatting | bytes 65536
  42.5 1.2 %copy.16 = f32[256]{0:T(256)} copy(f32[256]{0:T(256)} %bitcast.13) | data formatting | bytes 2048
  43.8 1.2 %copy.17 = f32[256]{0:T(256)} copy(f32[256]{0:T(256)} %bitcast.12) | data formatting | bytes 2048

commit v2 on v1

--- a/solution.py
+++ b/solution.py
@@ -22,20 +22,34 @@
     return lax.dot_general(a, b, (((1,), (1,)), ((), ())), preferred_element_type=F32)
 
 
-def dot_full(a, b):
-    return lax.dot_general(
-        a,
-        b,
-        (((1,), (0,)), ((), ())),
-        preferred_element_type=F32,
-        precision=lax.Precision.HIGHEST,
-    )
-
-
-def iterations(features):
-    low = 1.0 / (1.0 + features / REG)
+def dot_plain(a, b):
+    return lax.dot_general(a, b, (((1,), (0,)), ((), ())), preferred_element_type=F32)
+
+
+def parts(x):
+    one = x.astype(BF16)
+    rest = x - one.astype(F32)
+    two = rest.astype(BF16)
+    return one, two, (rest - two.astype(F32)).astype(BF16)
+
+
+def as_left(p):
+    return jnp.concatenate([p[0], p[1]], axis=1), jnp.concatenate([p[0], p[2]], axis=1)
+
+
+def as_right(p):
+    pair = jnp.concatenate([p[0], p[1]], axis=1)
+    return jnp.concatenate([pair, pair], axis=0), jnp.concatenate([p[2], p[0]], axis=0)
+
+
+def dot_full(left, right):
+    wide = dot_plain(left[0], right[0])
+    return wide[:, :BLOCK] + (wide[:, BLOCK:] + dot_plain(left[1], right[1]))
+
+
+def iterations(low, goal):
     count = 0
-    while low < 1.0 - 1e-6:
+    while low < goal:
         low = 4.0 * low / (1.0 + low) ** 2
         count += 1
     return count
@@ -64,7 +78,7 @@
 def kernel(
     groups,
     owners,
-    rounds,
+    features,
     counts_ref,
     order_ref,
     x_hbm,
@@ -196,14 +210,6 @@
     y_col = [to_col(r, eye) for r in y_row]
     b_col = [to_col(r, eye) for r in b_row]
 
-    others(lambda p: recv_from(0, p, cnt_all.at[p]).wait_recv())
-    cnt_all[me] = cnt_mine[...]
-    live_blocks = lax.fori_loop(
-        0, groups, lambda i, acc: acc + cnt_all[i], jnp.zeros((1, LANES), F32)
-    )
-    samples_total = live_blocks * BLOCK
-    scale = groups / (REG * samples_total)
-
     feat_copy.wait()
     full = gram_mine[...] + gram_other[...]
     first = full[rows : rows + 1, :] + full[rows + 1 : rows + 2, :]
@@ -221,28 +227,54 @@
         for a in range(CAP)
     ]
 
-    systems, carry = [], []
-    for v in range(CAP):
-        system = jnp.where(eye, 1.0, 0.0) + scale * grams[v][v]
-        top = jnp.max(jnp.sum(jnp.abs(system), axis=0, keepdims=True), axis=1, keepdims=True)
-        low = 1.0 / top
-        step = 2.0 / (1.0 + low) * low
-        carry.append(step * (jnp.where(eye, 2.0, 0.0) - step * system))
-        carry.append(4.0 * low / ((1.0 + low) * (1.0 + low)))
-        systems.append(system)
-
-    def improve(_, state):
+    diag = jnp.where(eye, 1.0, 0.0)
+    ratio = (CAP * groups / (groups + 1)) ** 0.5
+    middle = groups / (REG * BLOCK * CAP * groups) * ratio
+    rounds = iterations(1.0 / (1.0 + middle * features * BLOCK), 0.99)
+    refines = iterations(0.99 / ratio, 1.0 - 1e-6)
+
+    def improve(lefts, state):
         new = []
         for v in range(CAP):
             inverse, low = state[2 * v], state[2 * v + 1]
             mu = 2.0 / (1.0 + low)
-            near = dot_full(systems[v], inverse)
-            new.append(mu * (2.0 * inverse - mu * dot_full(inverse, near)))
+            terms = parts(inverse)
+            near = dot_full(lefts[v], as_right(terms))
+            far = dot_full(as_left(terms), as_right(parts(near)))
+            new.append(mu * (2.0 * inverse - mu * far))
             new.append(low * mu * mu)
         return tuple(new)
 
-    carry = lax.fori_loop(1, rounds, improve, tuple(carry))
-    inverses = [carry[2 * v] for v in range(CAP)]
+    lefts, carry = [], []
+    for v in range(CAP):
+        system = diag + middle * grams[v][v]
+        top = jnp.max(jnp.sum(jnp.abs(system), axis=0, keepdims=True), axis=1, keepdims=True)
+        low = 1.0 / top
+        step = 2.0 / (1.0 + low) * low
+        carry.append(step * (2.0 * diag - step * system))
+        carry.append(4.0 * low / ((1.0 + low) * (1.0 + low)))
+        lefts.append(as_left(parts(system)))
+    carry = lax.fori_loop(1, rounds, lambda _, state: improve(lefts, state), tuple(carry))
+
+    others(lambda p: recv_from(0, p, cnt_all.at[p]).wait_recv())
+    cnt_all[me] = cnt_mine[...]
+    live_blocks = lax.fori_loop(
+        0, groups, lambda i, acc: acc + cnt_all[i], jnp.zeros((1, LANES), F32)
+    )
+    samples_total = live_blocks * BLOCK
+    scale = groups / (REG * samples_total)
+
+
+    quotient = scale[:, 0:1] / middle
+    start = 0.99 * jnp.minimum(quotient, 1.0 / quotient)
+    state = []
+    for v in range(CAP):
+        state.append(carry[2 * v] / jnp.maximum(quotient, 1.0))
+        state.append(start)
+    lefts = [as_left(parts(diag + scale * grams[v][v])) for v in range(CAP)]
+    for _ in range(refines):
+        state = improve(lefts, state)
+    inverses = [state[2 * v] for v in range(CAP)]
 
     moved = [None] * CAP
     for j in range(PASSES * CAP):
@@ -354,6 +386,12 @@
     others(drain)
 
 
+def hand_over(*refs):
+    count = len(refs) // 2
+    for source, target in zip(refs[:count], refs[count:]):
+        target[...] = source[...]
+
+
 def body(groups, features, samples, labels, dual, counts, order, weights):
     rows, half = samples.shape
     owners = min(groups, half // LANES)
@@ -362,7 +400,7 @@
     smem = pl.BlockSpec(memory_space=pltpu.SMEM)
     tall = rows + 16
     wn, dn, mg, gap = pl.pallas_call(
-        functools.partial(kernel, groups, owners, iterations(features)),
+        functools.partial(kernel, groups, owners, features),
         out_shape=(
             jax.ShapeDtypeStruct((owners, 1, chunk), F32),
             jax.ShapeDtypeStruct((CAP, BLOCK), F32),
@@ -400,6 +438,13 @@
         labels.reshape(CAP, BLOCK),
         dual.reshape(CAP, BLOCK),
     )
+    results = (wn, dn, mg, gap)
+    wn, dn, mg, gap = pl.pallas_call(
+        hand_over,
+        out_shape=tuple(jax.ShapeDtypeStruct(r.shape, r.dtype) for r in results),
+        in_specs=[vmem] * len(results),
+        out_specs=(vmem,) * len(results),
+    )(*results)
     return (wn.reshape(half), dn.reshape(rows), mg.reshape(rows), gap[0, 0])
 
 

time: 47 us -> 42 us (0.89)
  local copies, waits for them, and re-layouts: 3.8 us -> 0 us
  between operations: 3.03 us -> 1.29 us
  Pallas kernels: 39.9 us -> 40.4 us
    unnamed x3 -> x0, local copies, waits for them, and re-layouts: 3.8 us -> none
    pallas_call x1 -> x2, Pallas kernels: 39.9 us -> 40.4 us  [the longest x1 39 us: body(): pl.pallas_call(functools.partial(kernel, groups, owners, features), out_s...]
where the time goes in v2:
time: 42 us; the launch traced here: 41.7 us
  Pallas kernels  40.4 us (96%)
  between operations  1.29 us (3%)
    pallas_call x1, Pallas kernels, body(): pl.pallas_call(functools.partial(kernel, groups, owners, features), out_s...  39 us
    pallas_call x1, Pallas kernels, body(): pl.pallas_call(hand_over, out_shape=tuple((jax.ShapeDtypeStruct(r.shape,...  1.4 us

profile of v2, /device:TPU:0, one launch (start us, length us, event | category | flops | bytes accessed | tf_op | source)
XLA Modules:
  0.0 41.7 jit_solution(10390692276502753189)
XLA Ops:
  1.3 39.0 %shard_map.93 = (f32[16,1,512]{2,1,0:T(1,128)}, f32[2,128]{1,0:T(2,128)}, f32[2,128]{1,0:T(2,128)}, f32[1,128]{1,0:T(1,128)}) custom-call(s32[1]{0:T(128)S(6)} %copy.10.counts_ref, s32[1,2]{1,0:T(1,128)} %order_ref.1, bf16[256,8192]{1,0:T(8,128)(2,1)} %x_hbm.1, f32[1,8192]{1,0:T(1,128)} %bitcast.8, s32[2,128]{1,0:T(2,128)} %bitcast.9, f32[2,128]{1,0:T(2,128)} %bitcast.10), custom_call_target="tpu_custom_call" | custom-call | tf_op jit(solution)/shard_map/pallas_call | solution.py:402
  40.3 1.4 %shard_map.94 = (f32[16,1,512]{2,1,0:T(1,128)}, f32[2,128]{1,0:T(2,128)}, f32[2,128]{1,0:T(2,128)}, f32[1,128]{1,0:T(1,128)}) custom-call(f32[16,1,512]{2,1,0:T(1,128)} %get-tuple-element.12.refs_0_, f32[2,128]{1,0:T(2,128)} %get-tuple-element.13.refs_1_, f32[2,128]{1,0:T(2,128)} %get-tuple-element.14.refs_2_, f32[1,128]{1,0:T(1,128)} %get-tuple-element.15.refs_3_), custom_call_target="tpu_custom_call" | custom-call | tf_op jit(solution)/shard_map/pallas_call | solution.py:442

commit v3 on v2

--- a/solution.py
+++ b/solution.py
@@ -42,8 +42,10 @@
     return jnp.concatenate([pair, pair], axis=0), jnp.concatenate([p[2], p[0]], axis=0)
 
 
-def dot_full(left, right):
+def dot_full(left, right, short):
     wide = dot_plain(left[0], right[0])
+    if short:
+        return wide[:, :BLOCK] + wide[:, BLOCK:]
     return wide[:, :BLOCK] + (wide[:, BLOCK:] + dot_plain(left[1], right[1]))
 
 
@@ -233,14 +235,14 @@
     rounds = iterations(1.0 / (1.0 + middle * features * BLOCK), 0.99)
     refines = iterations(0.99 / ratio, 1.0 - 1e-6)
 
-    def improve(lefts, state):
+    def improve(lefts, state, short=False):
         new = []
         for v in range(CAP):
             inverse, low = state[2 * v], state[2 * v + 1]
             mu = 2.0 / (1.0 + low)
             terms = parts(inverse)
-            near = dot_full(lefts[v], as_right(terms))
-            far = dot_full(as_left(terms), as_right(parts(near)))
+            near = dot_full(lefts[v], as_right(terms), short)
+            far = dot_full(as_left(terms), as_right(parts(near)), short)
             new.append(mu * (2.0 * inverse - mu * far))
             new.append(low * mu * mu)
         return tuple(new)
@@ -254,7 +256,8 @@
         carry.append(step * (2.0 * diag - step * system))
         carry.append(4.0 * low / ((1.0 + low) * (1.0 + low)))
         lefts.append(as_left(parts(system)))
-    carry = lax.fori_loop(1, rounds, lambda _, state: improve(lefts, state), tuple(carry))
+    for k in range(1, rounds):
+        carry = improve(lefts, carry, short=k <= 5)
 
     others(lambda p: recv_from(0, p, cnt_all.at[p]).wait_recv())
     cnt_all[me] = cnt_mine[...]

time: 42 us -> 40.5 us (0.964)
  Pallas kernels: 40.4 us -> 39 us
    pallas_call x1, Pallas kernels: 39 us -> 37.6 us  [body(): pl.pallas_call(functools.partial(kernel, groups, owners, features), out_s...]
where the time goes in v3:
time: 40.5 us; the launch traced here: 40.3 us
  Pallas kernels  39 us (96%)
  between operations  1.29 us (3%)
    pallas_call x1, Pallas kernels, body(): pl.pallas_call(functools.partial(kernel, groups, owners, features), out_s...  37.6 us
    pallas_call x1, Pallas kernels, body(): pl.pallas_call(hand_over, out_shape=tuple((jax.ShapeDtypeStruct(r.shape,...  1.4 us

profile of v3, /device:TPU:0, one launch (start us, length us, event | category | flops | bytes accessed | tf_op | source)
XLA Modules:
  0.0 40.3 jit_solution(10948840635624072532)
XLA Ops:
  1.3 37.6 %shard_map.93 = (f32[16,1,512]{2,1,0:T(1,128)}, f32[2,128]{1,0:T(2,128)}, f32[2,128]{1,0:T(2,128)}, f32[1,128]{1,0:T(1,128)}) custom-call(s32[1]{0:T(128)S(6)} %copy.10.counts_ref, s32[1,2]{1,0:T(1,128)} %order_ref.1, bf16[256,8192]{1,0:T(8,128)(2,1)} %x_hbm.1, f32[1,8192]{1,0:T(1,128)} %bitcast.8, s32[2,128]{1,0:T(2,128)} %bitcast.9, f32[2,128]{1,0:T(2,128)} %bitcast.10), custom_call_target="tpu_custom_call" | custom-call | tf_op jit(solution)/shard_map/pallas_call | solution.py:405
  38.9 1.4 %shard_map.94 = (f32[16,1,512]{2,1,0:T(1,128)}, f32[2,128]{1,0:T(2,128)}, f32[2,128]{1,0:T(2,128)}, f32[1,128]{1,0:T(1,128)}) custom-call(f32[16,1,512]{2,1,0:T(1,128)} %get-tuple-element.12.refs_0_, f32[2,128]{1,0:T(2,128)} %get-tuple-element.13.refs_1_, f32[2,128]{1,0:T(2,128)} %get-tuple-element.14.refs_2_, f32[1,128]{1,0:T(1,128)} %get-tuple-element.15.refs_3_), custom_call_target="tpu_custom_call" | custom-call | tf_op jit(solution)/shard_map/pallas_call | solution.py:445
